TPU v7x, 128 devices: a whole 4x4x4 slice. The times are simulated.
128 devices in a mesh: dp: 16 (over x_hi, z, core), tensor: 8 (over y, x_lo).
Axes of the slice: x: 4 (x_hi: 2, x_lo: 2; x = x_hi * 2 + x_lo), y: 4, z: 4, core: 2. Of those that a mesh axis runs over, the one named last changes fastest.
Arguments:
- latents: bfloat16 [176, 256, 640], P('dp', 'tensor'), may hold values from -6 to 6
- cotangent: bfloat16 [176, 256, 640], P('dp', 'tensor'), may hold values from -6 to 6
- trunc_steps: int32 [16], replicated, may hold values from 30 to 40, as said below
- timesteps: int32 [176], replicated, may hold values from 100 to 900
- tile_map: int32 [176], replicated, may hold values from 0 to 175, as said below
- gain: float32 [640], replicated, may hold values from 0.5 to 1.5
- w_value: bfloat16 [640, 2560], P(None, 'tensor'), may hold values from -0.25 to 0.25
- w_gate: bfloat16 [640, 2560], P(None, 'tensor'), may hold values from -0.25 to 0.25
- w_out: bfloat16 [640, 2560], P(None, 'tensor'), may hold values from -0.125 to 0.125
Outputs:
- placed_grad: bfloat16 [176, 256, 640], P('dp', 'tensor')
- grad_value: float32 [640, 2560], P('dp', 'tensor')
- grad_gate: float32 [640, 2560], P('dp', 'tensor')
- grad_out_proj: float32 [640, 2560], P('dp', 'tensor')
- grad_gain: float32 [640], replicated
Inputs may be any that keep to these rules, and one draw needn't show every extreme that they name: trunc_steps lies in 30 to 40, so a prompt has 1 to 11 live slots, its lowest ones. tile_map is a permutation of 0 to 175. Output slots g * 11 to g * 11 + 10 form group g; the live items go to the lowest slots of the groups, and each group receives the floor or the ceiling of (number of live items) / 16 of them.
All inputs are finite; a program needn't handle non-finite values.
Results may differ from a plain program's by a relative error of at most 0.0068.
Values may be sent and summed in bfloat16 or wider, within the bound.
A program may use at most 64 MiB of HBM per device.

v0:
```python
import functools
import jax
import jax.numpy as jnp
from jax import lax
from jax.sharding import Mesh
from jax.sharding import PartitionSpec as P

TENSOR = ("tensor_0", "tensor_1")
DP = ("dp_0", "dp_1", "dp_2")
DP_TENSOR = ("dp_0", "dp_1", "dp_2", "tensor_0", "tensor_1")
eps = 1e-05


def sent_together(arrays, axis, dim, along):
    widths = [a.shape[along] for a in arrays]
    both = jnp.concatenate(arrays, axis=along)
    whole = lax.all_gather(both, axis, axis=dim, tiled=True)
    return tuple(jnp.split(whole, [sum(widths[:k]) for k in range(1, len(widths))], axis=along))


def sum_by_axis(x, axes, dim):
    for axis in axes:
        x = lax.psum_scatter(x, axis, scatter_dimension=dim, tiled=True)
    return x


def in_one_piece(arrays, axis, dim, along):
    both = jnp.concatenate(arrays, axis=along)
    whole, at, gathered = (lax.psum_scatter(both, axis, scatter_dimension=dim, tiled=True), 0, [])
    for a in arrays:
        gathered.append(lax.slice_in_dim(whole, at, at + a.shape[along], axis=along))
        at += a.shape[along]
    return tuple(gathered)


def one_axis_at_a_time(x, axes):
    return functools.reduce(lax.psum, axes, x)


def alpha_bars():
    betas = jnp.linspace(0.00085**0.5, 0.012**0.5, 1000, dtype=jnp.float32) ** 2
    return jnp.exp(jnp.cumsum(jnp.log1p(-betas)))


def gelu_parts(inputs):
    cdf = 0.5 * (1.0 + lax.erf(inputs * 0.7071067811865476))
    density = jnp.exp(-0.5 * inputs * inputs) * 0.3989422804014327
    return (inputs * cdf, cdf + inputs * density)


def norm_backward(d_normed, grad_part, hat_part, inv_part, gain):
    d_hat = d_normed * gain
    input_grad = grad_part.astype(jnp.float32) + inv_part * (
        d_hat
        - jnp.mean(d_hat, axis=-1, keepdims=True)
        - hat_part * jnp.mean(d_hat * hat_part, axis=-1, keepdims=True)
    )
    gain_local = jnp.sum(d_normed * hat_part, axis=(0, 1))
    return (input_grad, gain_local)


def tile_backward(tiles, cot_tiles, slot_times, live_count, gain, w_value, w_gate, w_out):
    full_x, full_cot = sent_together((tiles, cot_tiles), TENSOR, 1, 0)
    width = full_x.shape[2]
    local_rows = tiles.shape[1]
    inner = w_value.shape[1]
    slot_total = full_x.shape[0]
    table = alpha_bars()
    picked = jnp.sum(
        jnp.where(
            slot_times[:, None] == jnp.arange(1000, dtype=jnp.int32)[None, :], table[None, :], 0.0
        ),
        axis=1,
    )
    noise_scale = jnp.sqrt(1.0 - picked)
    x_float = full_x.astype(jnp.float32)
    row_mean = jnp.mean(x_float, axis=-1, keepdims=True)
    centred = x_float - row_mean
    row_var = jnp.mean(centred * centred, axis=-1, keepdims=True)
    inv_std = lax.rsqrt(row_var + eps)
    x_hat = centred * inv_std
    normed = (x_hat * gain).astype(jnp.bfloat16)
    grad_tile = (full_cot.astype(jnp.float32) * noise_scale[:, None, None]).astype(jnp.bfloat16)
    first_dims = (((0,), (0,)), ((), ()))
    last_dims = (((1,), (1,)), ((), ()))

    def one_slot(slot_idx, carry):
        acc_wv, acc_wg, acc_wo, normed_buf = carry
        norm_tile = lax.dynamic_index_in_dim(normed, slot_idx, 0, keepdims=False)
        grad_one = lax.dynamic_index_in_dim(grad_tile, slot_idx, 0, keepdims=False)
        values_proj = jnp.dot(norm_tile, w_value, preferred_element_type=jnp.float32)
        gate_proj = jnp.dot(norm_tile, w_gate, preferred_element_type=jnp.float32)
        gelu_gate, gelu_slope = gelu_parts(gate_proj)
        hidden = (values_proj * gelu_gate).astype(jnp.bfloat16)
        d_hidden = jnp.dot(grad_one, w_out, preferred_element_type=jnp.float32)
        d_value = (d_hidden * gelu_gate).astype(jnp.bfloat16)
        d_gate = (d_hidden * values_proj * gelu_slope).astype(jnp.bfloat16)
        acc_wv = acc_wv + lax.dot_general(
            norm_tile, d_value, first_dims, preferred_element_type=jnp.float32
        )
        acc_wg = acc_wg + lax.dot_general(
            norm_tile, d_gate, first_dims, preferred_element_type=jnp.float32
        )
        acc_wo = acc_wo + lax.dot_general(
            grad_one, hidden, first_dims, preferred_element_type=jnp.float32
        )
        d_normed = lax.dot_general(d_value, w_value, last_dims, preferred_element_type=jnp.float32)
        d_normed = d_normed + lax.dot_general(
            d_gate, w_gate, last_dims, preferred_element_type=jnp.float32
        )
        normed_buf = lax.dynamic_update_index_in_dim(normed_buf, d_normed, slot_idx, 0)
        return (acc_wv, acc_wg, acc_wo, normed_buf)

    zero_w = jnp.zeros((width, inner), jnp.float32)
    init = (zero_w, zero_w, zero_w, jnp.zeros(full_x.shape, jnp.float32))
    acc_wv, acc_wg, acc_wo, normed_buf = lax.fori_loop(0, live_count, one_slot, init)
    offset = lax.axis_index(TENSOR) * local_rows
    hat_part = lax.dynamic_slice_in_dim(x_hat, offset, local_rows, 1)
    inv_part = lax.dynamic_slice_in_dim(inv_std, offset, local_rows, 1)
    grad_part = lax.dynamic_slice_in_dim(grad_tile, offset, local_rows, 1)
    slot_live = (jnp.arange(slot_total, dtype=jnp.int32) < live_count)[:, None, None]
    d_normed = sum_by_axis(normed_buf, TENSOR, 1)
    input_grad, gain_local = norm_backward(d_normed, grad_part, hat_part, inv_part, gain)
    input_grad = jnp.where(slot_live, input_grad, 0.0).astype(jnp.bfloat16)
    return (input_grad, (acc_wv, acc_wg, acc_wo), gain_local)


def per_device(latents, cotangent, trunc_steps, timesteps, tile_map, gain, w_value, w_gate, w_out):
    slot_total = latents.shape[0]
    total = tile_map.shape[0]
    my_group = lax.axis_index(DP)
    item_ids = jnp.arange(total, dtype=jnp.int32)
    live_all = (item_ids % slot_total < jnp.repeat(trunc_steps, slot_total) - 29).astype(jnp.int32)
    my_slots = my_group * slot_total + jnp.arange(slot_total, dtype=jnp.int32)
    is_mine = tile_map[:, None] == my_slots[None, :]
    dest_source = jnp.sum(jnp.where(is_mine, item_ids[:, None], 0), axis=0)
    slot_times = jnp.take(timesteps, my_slots)
    live_count = jnp.sum(jnp.take(live_all, my_slots))
    own_grad, weight_parts, gain_local = tile_backward(
        latents, cotangent, slot_times, live_count, gain, w_value, w_gate, w_out
    )
    every_grad = lax.all_gather(own_grad, DP, axis=0, tiled=True)
    placed_grad = jnp.take(every_grad, dest_source, axis=0)
    grad_value, grad_gate, grad_out_proj = in_one_piece(
        (weight_parts[0], weight_parts[1], weight_parts[2]), DP, 0, 1
    )
    grad_gain = one_axis_at_a_time(gain_local, DP_TENSOR)
    return (placed_grad, grad_value, grad_gate, grad_out_proj, grad_gain)


def solution(mesh):
    split = Mesh(
        mesh.devices.reshape(2, 4, 2, 4, 2), ("dp_0", "dp_1", "dp_2", "tensor_0", "tensor_1")
    )
    in_specs = (
        P(DP, TENSOR, None),
        P(DP, TENSOR, None),
        P(),
        P(),
        P(),
        P(),
        P(None, TENSOR),
        P(None, TENSOR),
        P(None, TENSOR),
    )
    out_specs = (P(DP, TENSOR, None), P(DP, TENSOR), P(DP, TENSOR), P(DP, TENSOR), P())
    return jax.shard_map(
        per_device, mesh=split, in_specs=in_specs, out_specs=out_specs, check_vma=False
    )
```

profile of v0, /device:TPU:1, one launch (start us, length us, event | category | flops | bytes accessed | tf_op | source)
XLA Modules:
  0.0 555.5 jit_solution(6888655949699349684)
XLA Ops:
  7.2 2.2 pad_maximum_fusion.1
  13.2 145.6 %all-gather.3.cloned.1.call-done = bf16[22,256,640]{2,1,0:T(8,128)(2,1)} async-done(((bf16[22,32,640]{2,1,0:T(8,128)(2,1)}), bf16[22,256,640]{2,1,0:T(8,128)(2,1)}) %all-gather.3.cloned.1.call-update) | async-done | bytes 7208976 | tf_op jit(solution)/shard_map/all_gather | solution.py:17
  158.9 2.7 convert_reduce_fusion
  161.6 3.2 fusion.34
  164.9 6.2 %fusion.32 = (f32[11,256,640]{2,1,0:T(8,128)}, bf16[11,256,640]{2,1,0:T(8,128)(2,1)}, bf16[11,256,640]{2,1,0:T(8,128)(2,1)}) fusion(f32[11,256]{1,0:T(8,128)S(1)} %add_rsqrt_fusion, f32[11,256]{1,0:T(8,128)S(1)} %broadcast_multiply_fusion, bf16[22,256,640]{2,1,0:T(8,128)(2,1)S(1)} %copy-done.3, f32[640]{0:T(1024)S(1)} %copy-done.4, f32[11]{0:T(128)S(1)} %subtract_sqrt_fusion), kind=kLoop, calls=%fused_computation.43 | loop fusion | flops 14417920 | bytes 21652012 | tf_op jit(solution)/shard_map/mul | solution.py:81
  171.3 3.6 broadcast_in_dim.86
  174.9 94.7 %while.16 = (s32[]{:T(128)}, f32[640,320]{0,1:T(8,128)S(1)}, f32[640,320]{0,1:T(8,128)S(1)}, f32[640,320]{0,1:T(8,128)S(1)}, f32[11,256,640]{2,1,0:T(8,128)}, /*...) while((s32[]{:T(128)}, f32[640,320]{0,1:T(8,128)S(1)}, ...), condition=%wide.region_8.10_spmd, body=%wide.region_7.9_spmd.sunk | while | flops 842424320 | bytes 15319243 | solution.py:116
  199.1 1.4 multiply_convert_fusion.8
  220.0 1.4 multiply_convert_fusion.8
  240.9 1.4 multiply_convert_fusion.8
  269.7 92.8 %reduce-scatter.4.cloned.1.call-done = f32[11,64,640]{2,1,0:T(8,128)} async-done(((f32[11,256,640]{2,1,0:T(8,128)}), f32[11,64,640]{2,1,0:T(8,128)}) %reduce-scatter.4.cloned.1.call-update) | async-done | bytes 1802256 | tf_op jit(solution)/shard_map/reduce_scatter | solution.py:23
  364.6 3.3 pad_maximum_fusion
  368.7 27.1 %reduce-scatter.6.cloned.1.call-done = f32[11,32,640]{2,1,0:T(8,128)} async-done(((f32[11,64,640]{2,1,0:T(8,128)}), f32[11,32,640]{2,1,0:T(8,128)}) %reduce-scatter.6.cloned.1.call-update) | async-done | bytes 901136 | tf_op jit(solution)/shard_map/reduce_scatter | solution.py:23
  395.7 1.8 multiply_reduce_fusion
  397.5 2.7 select_convert_fusion
  400.4 72.0 %reduce-scatter.8.cloned.1.call-done = f32[40,960]{1,0:T(8,128)} async-done(((f32[640,960]{1,0:T(8,128)}), f32[40,960]{1,0:T(8,128)}) %reduce-scatter.8.cloned.1.call-update) | async-done | bytes 153616 | tf_op jit(solution)/shard_map/reduce_scatter | solution.py:29
  472.4 1.6 fusion.41
  474.0 5.3 psum.35
  479.3 8.1 %psum.36 = f32[640]{0:T(1024)S(1)} all-reduce(f32[640]{0:T(1024)S(1)} %psum.35), channel_id=1, replica_groups=mesh['dp_0'=2,'dp_1'=4,'dp_2'=2,'tensor_0'=4,'tensor_1'=2] {'dp_1'}, use_global_device_ids=true, to_apply=%region_16.18 | all-reduce | flops 640 | bytes 5120 | tf_op jit(solution)/shard_map/psum | solution.py:37
  487.4 8.1 %psum.37 = f32[640]{0:T(1024)S(1)} all-reduce(f32[640]{0:T(1024)S(1)} %psum.36), channel_id=1, replica_groups=mesh['dp_0'=2,'dp_1'=4,'dp_2'=2,'tensor_0'=4,'tensor_1'=2] {'dp_2'}, use_global_device_ids=true, to_apply=%region_17.19 | all-reduce | flops 640 | bytes 5120 | tf_op jit(solution)/shard_map/psum | solution.py:37
  495.5 8.8 %psum.38 = f32[640]{0:T(1024)S(1)} all-reduce(f32[640]{0:T(1024)S(1)} %psum.37), channel_id=1, replica_groups=mesh['dp_0'=2,'dp_1'=4,'dp_2'=2,'tensor_0'=4,'tensor_1'=2] {'tensor_0'}, use_global_device_ids=true, to_apply=%region_18.20 | all-reduce | flops 640 | bytes 5120 | tf_op jit(solution)/shard_map/psum | solution.py:37
  504.4 4.4 psum.39
  508.7 35.7 %all-gather.5.cloned.1.call-done = bf16[176,32,640]{2,1,0:T(8,128)(2,1)} async-done(((bf16[11,32,640]{2,1,0:T(8,128)(2,1)}), bf16[176,32,640]{2,1,0:T(8,128)(2,1)}) %all-gather.5.cloned.1.call-update) | async-done | bytes 7208976 | tf_op jit(solution)/shard_map/all_gather | solution.py:142
  544.4 3.7 gather_fusion
  (129 shorter events, 91.3 us)
Async XLA Ops:
  7.2 3.7 copy-start
  7.2 157.7 %copy-start.4 = (f32[640]{0:T(1024)S(1)}, f32[640]{0:T(1024)}, u32[]{:S(2)}) copy-start(f32[640]{0:T(1024)} %param.18) | copy-start | bytes 7684
  7.2 151.7 %all-gather.3.cloned.1.call-start = ((), (), s32[]{:S(2)}) async-start(), calls=%async_computation.3 | async-start | bytes 8110080 | tf_op jit(solution)/shard_map/all_gather | solution.py:17
  9.4 353.1 %reduce-scatter.4.cloned.1.call-start = ((), (), s32[]{:S(2)}) async-start(), calls=%async_computation.4 | async-start | bytes 9011200 | tf_op jit(solution)/shard_map/reduce_scatter | solution.py:23
  158.9 6.0 %copy-start.3 = (bf16[22,256,640]{2,1,0:T(8,128)(2,1)S(1)}, bf16[22,256,640]{2,1,0:T(8,128)(2,1)}, u32[]{:S(2)}) copy-start(bf16[22,256,640]{2,1,0:T(8,128)(2,1)} %all-gather.3.cloned.1.call-done) | copy-start | bytes 21626884
  171.1 3.8 copy-start.1
  171.1 3.8 copy-start.2
  269.6 126.1 %reduce-scatter.6.cloned.1.call-start = ((), (), s32[]{:S(2)}) async-start(), calls=%async_computation.5 | async-start | bytes 2703360 | tf_op jit(solution)/shard_map/reduce_scatter | solution.py:23
  362.5 109.9 %reduce-scatter.8.cloned.1.call-start = ((), (), s32[]{:S(2)}) async-start(), calls=%async_computation.7 | async-start | bytes 2785280 | tf_op jit(solution)/shard_map/reduce_scatter | solution.py:29
  364.2 36.0 %copy-start.5 = (s32[176]{0:T(256)S(1)}, s32[176]{0:T(256)}, u32[]{:S(2)}) copy-start(s32[176]{0:T(256)} %param.17) | copy-start | bytes 2116
  367.9 176.5 %all-gather.5.cloned.1.call-start = ((), (), s32[]{:S(2)}) async-start(), calls=%async_computation.6 | async-start | bytes 7659520 | tf_op jit(solution)/shard_map/all_gather | solution.py:142
Sparse Core Ops, SparseCore 0:
  9.6 149.1 all-gather.2
  269.8 92.7 reduce-scatter.3
  364.9 30.7 reduce-scatter.5
  399.6 72.7 reduce-scatter.7
  475.3 69.0 all-gather.4
where the time goes:
time: 558 us; the launch traced here: 555 us
  waiting for transfers between devices  373 us (67%)
  matrix products  87.6 us (16%)
  blocking collectives  34.7 us (6%)
  other arithmetic  25.8 us (5%)
  between operations  14 us (3%)
  local copies, waits for them, and re-layouts  12.8 us (2%)
  loops' own time  7.12 us (1%)
    all_gather x1, waiting for transfers between devices, sent_together(): whole = lax.all_gather(both, axis, axis=dim, tiled=True)  146 us
    reduce_scatter x2, waiting for transfers between devices, sum_by_axis(): x = lax.psum_scatter(x, axis, scatter_dimension=dim, tiled=True)  120 us
    reduce_scatter x1, waiting for transfers between devices, in_one_piece(): lax.psum_scatter(both, axis, scatter_dimension=dim, tiled=True)  72 us
    all_gather x1, waiting for transfers between devices, per_device(): every_grad = lax.all_gather(own_grad, DP, axis=0, tiled=True)  35.7 us
    psum x5, blocking collectives, one_axis_at_a_time(): return functools.reduce(lax.psum, axes, x)  34.7 us
    dot_general x9, matrix products, one_slot(): d_hidden = jnp.dot(grad_one, w_out, preferred_element_type=jnp.float32)  12.9 us
    dot_general x9, matrix products, one_slot(): lax.dot_general(norm_tile, d_gate, first_dims, preferred_element_type=jnp...  12.4 us
    dot_general x9, matrix products, one_slot(): lax.dot_general(grad_one, hidden, first_dims, preferred_element_type=jnp....  12.2 us
  transfers between devices with their start and end apart: 5, of which 5 were waited for; matrix products, arithmetic and copies ran while one was open for 3% of the time, Pallas kernels for 0%

commit v1 on v0

--- a/solution.py
+++ b/solution.py
@@ -139,7 +139,9 @@
     own_grad, weight_parts, gain_local = tile_backward(
         latents, cotangent, slot_times, live_count, gain, w_value, w_gate, w_out
     )
-    every_grad = lax.all_gather(own_grad, DP, axis=0, tiled=True)
+    every_grad = jnp.concatenate(
+        lax.all_to_all(jnp.stack([own_grad] * lax.axis_size(DP)), DP, 0, 0), axis=0
+    )
     placed_grad = jnp.take(every_grad, dest_source, axis=0)
     grad_value, grad_gate, grad_out_proj = in_one_piece(
         (weight_parts[0], weight_parts[1], weight_parts[2]), DP, 0, 1

time: 558 us -> 581 us (1.041)
  waiting for transfers between devices: 373 us -> 385 us
  starting transfers between devices: 0.2 us -> 7.57 us
    reduce_scatter x1, waiting for transfers between devices: 72 us -> 114 us  [in_one_piece(): lax.psum_scatter(both, axis, scatter_dimension=dim, tiled=True)]
    all_gather x1 -> x0, waiting for transfers between devices: 35.7 us -> none  [per_device(): every_grad = lax.all_gather(own_grad, DP, axis=0, tiled=True)]
    all_to_all x0 -> x1, starting transfers between devices: none -> 7.41 us  [per_device(): lax.all_to_all(jnp.stack([own_grad] * lax.axis_size(DP)), DP, 0, 0)]
  transfers between devices with their start and end apart: 5 -> 5, of which waited for: 5 -> 4; matrix products, arithmetic and copies ran while one was open for 3% -> 2% of each run, Pallas kernels for 0% -> 0%
where the time goes in v1:
time: 581 us; the launch traced here: 576 us
  waiting for transfers between devices  385 us (66%)
  matrix products  87.6 us (15%)
  blocking collectives  33.5 us (6%)
  other arithmetic  25 us (4%)
  local copies, waits for them, and re-layouts  16.4 us (3%)
  between operations  14 us (2%)
  starting transfers between devices  7.57 us (1%)
  loops' own time  7.12 us (1%)
    all_gather x1, waiting for transfers between devices, sent_together(): whole = lax.all_gather(both, axis, axis=dim, tiled=True)  146 us
    reduce_scatter x2, waiting for transfers between devices, sum_by_axis(): x = lax.psum_scatter(x, axis, scatter_dimension=dim, tiled=True)  125 us
    reduce_scatter x1, waiting for transfers between devices, in_one_piece(): lax.psum_scatter(both, axis, scatter_dimension=dim, tiled=True)  114 us
    psum x5, blocking collectives, one_axis_at_a_time(): return functools.reduce(lax.psum, axes, x)  33.5 us
    dot_general x9, matrix products, one_slot(): d_hidden = jnp.dot(grad_one, w_out, preferred_element_type=jnp.float32)  12.9 us
    dot_general x9, matrix products, one_slot(): lax.dot_general(norm_tile, d_gate, first_dims, preferred_element_type=jnp...  12.4 us
    dot_general x9, matrix products, one_slot(): lax.dot_general(grad_one, hidden, first_dims, preferred_element_type=jnp....  12.2 us
    dot_general x9, matrix products, one_slot(): lax.dot_general(d_gate, w_gate, last_dims, preferred_element_type=jnp.flo...  11.9 us
  transfers between devices with their start and end apart: 5, of which 4 were waited for; matrix products, arithmetic and copies ran while one was open for 2% of the time, Pallas kernels for 0%

profile of v1, /device:TPU:1, one launch (start us, length us, event | category | flops | bytes accessed | tf_op | source)
XLA Modules:
  0.0 576.2 jit_solution(11130507717078187981)
XLA Ops:
  7.2 2.2 pad_maximum_fusion.1
  13.3 145.6 %all-gather.2.cloned.1.call-done = bf16[22,256,640]{2,1,0:T(8,128)(2,1)} async-done(((bf16[22,32,640]{2,1,0:T(8,128)(2,1)}), bf16[22,256,640]{2,1,0:T(8,128)(2,1)}) %all-gather.2.cloned.1.call-update) | async-done | bytes 7208976 | tf_op jit(solution)/shard_map/all_gather | solution.py:17
  158.9 2.7 convert_reduce_fusion
  161.6 3.2 fusion.34
  164.9 6.2 %fusion.32 = (f32[11,256,640]{2,1,0:T(8,128)}, bf16[11,256,640]{2,1,0:T(8,128)(2,1)}, bf16[11,256,640]{2,1,0:T(8,128)(2,1)}) fusion(f32[11,256]{1,0:T(8,128)S(1)} %add_rsqrt_fusion, f32[11,256]{1,0:T(8,128)S(1)} %broadcast_multiply_fusion, bf16[22,256,640]{2,1,0:T(8,128)(2,1)S(1)} %copy-done.3, f32[640]{0:T(1024)S(1)} %copy-done.4, f32[11]{0:T(128)S(1)} %subtract_sqrt_fusion), kind=kLoop, calls=%fused_computation.43 | loop fusion | flops 14417920 | bytes 21652012 | tf_op jit(solution)/shard_map/mul | solution.py:81
  171.3 3.6 broadcast_in_dim.86
  174.9 94.7 %while.16 = (s32[]{:T(128)}, f32[640,320]{0,1:T(8,128)S(1)}, f32[640,320]{0,1:T(8,128)S(1)}, f32[640,320]{0,1:T(8,128)S(1)}, f32[11,256,640]{2,1,0:T(8,128)}, /*...) while((s32[]{:T(128)}, f32[640,320]{0,1:T(8,128)S(1)}, ...), condition=%wide.region_8.10_spmd, body=%wide.region_7.9_spmd.sunk | while | flops 842424320 | bytes 15319243 | solution.py:116
  178.2 1.4 multiply_convert_fusion.8
  240.9 1.4 multiply_convert_fusion.8
  269.7 92.8 %reduce-scatter.4.cloned.1.call-done = f32[11,64,640]{2,1,0:T(8,128)} async-done(((f32[11,256,640]{2,1,0:T(8,128)}), f32[11,64,640]{2,1,0:T(8,128)}) %reduce-scatter.4.cloned.1.call-update) | async-done | bytes 1802256 | tf_op jit(solution)/shard_map/reduce_scatter | solution.py:23
  363.3 32.5 %reduce-scatter.6.cloned.1.call-done = f32[11,32,640]{2,1,0:T(8,128)} async-done(((f32[11,64,640]{2,1,0:T(8,128)}), f32[11,32,640]{2,1,0:T(8,128)}) %reduce-scatter.6.cloned.1.call-update) | async-done | bytes 901136 | tf_op jit(solution)/shard_map/reduce_scatter | solution.py:23
  395.7 1.8 multiply_reduce_fusion
  397.5 1.9 select_convert_fusion
  399.4 3.5 stack.2
  403.0 7.4 %all-to-all-start = ((bf16[16,11,32,640]{3,2,1,0:T(8,128)(2,1)}), bf16[16,11,32,640]{3,2,1,0:T(8,128)(2,1)}, u32[]{:S(2)}, u32[]{:S(2)}) async-start(bf16[16,11,32,640]{3,2,1,0:T(8,128)(2,1)} %stack.2), calls=%async_computation.2 | async-start | bytes 14417920 | tf_op jit(solution)/shard_map/all_to_all | solution.py:143
  412.4 3.2 pad_maximum_fusion
  415.8 114.1 %reduce-scatter.8.cloned.1.call-done = f32[40,960]{1,0:T(8,128)} async-done(((f32[640,960]{1,0:T(8,128)}), f32[40,960]{1,0:T(8,128)}) %reduce-scatter.8.cloned.1.call-update) | async-done | bytes 153616 | tf_op jit(solution)/shard_map/reduce_scatter | solution.py:29
  529.9 1.6 fusion.41
  531.6 5.3 psum.35
  536.8 8.0 %psum.36 = f32[640]{0:T(1024)S(1)} all-reduce(f32[640]{0:T(1024)S(1)} %psum.35), channel_id=1, replica_groups=mesh['dp_0'=2,'dp_1'=4,'dp_2'=2,'tensor_0'=4,'tensor_1'=2] {'dp_1'}, use_global_device_ids=true, to_apply=%region_16.18 | all-reduce | flops 640 | bytes 5120 | tf_op jit(solution)/shard_map/psum | solution.py:37
  544.8 7.5 %psum.37 = f32[640]{0:T(1024)S(1)} all-reduce(f32[640]{0:T(1024)S(1)} %psum.36), channel_id=1, replica_groups=mesh['dp_0'=2,'dp_1'=4,'dp_2'=2,'tensor_0'=4,'tensor_1'=2] {'dp_2'}, use_global_device_ids=true, to_apply=%region_17.19 | all-reduce | flops 640 | bytes 5120 | tf_op jit(solution)/shard_map/psum | solution.py:37
  552.3 8.5 %psum.38 = f32[640]{0:T(1024)S(1)} all-reduce(f32[640]{0:T(1024)S(1)} %psum.37), channel_id=1, replica_groups=mesh['dp_0'=2,'dp_1'=4,'dp_2'=2,'tensor_0'=4,'tensor_1'=2] {'tensor_0'}, use_global_device_ids=true, to_apply=%region_18.20 | all-reduce | flops 640 | bytes 5120 | tf_op jit(solution)/shard_map/psum | solution.py:37
  560.7 4.4 psum.39
  565.1 3.7 gather_fusion
  (129 shorter events, 92.7 us)
Async XLA Ops:
  7.2 3.7 copy-start
  7.2 157.7 %copy-start.4 = (f32[640]{0:T(1024)S(1)}, f32[640]{0:T(1024)}, u32[]{:S(2)}) copy-start(f32[640]{0:T(1024)} %param.18) | copy-start | bytes 7684
  7.2 151.7 %all-gather.2.cloned.1.call-start = ((), (), s32[]{:S(2)}) async-start(), calls=%async_computation.4 | async-start | bytes 8110080 | tf_op jit(solution)/shard_map/all_gather | solution.py:17
  9.4 353.1 %reduce-scatter.4.cloned.1.call-start = ((), (), s32[]{:S(2)}) async-start(), calls=%async_computation.5 | async-start | bytes 9011200 | tf_op jit(solution)/shard_map/reduce_scatter | solution.py:23
  158.9 6.0 %copy-start.3 = (bf16[22,256,640]{2,1,0:T(8,128)(2,1)S(1)}, bf16[22,256,640]{2,1,0:T(8,128)(2,1)}, u32[]{:S(2)}) copy-start(bf16[22,256,640]{2,1,0:T(8,128)(2,1)} %all-gather.2.cloned.1.call-done) | copy-start | bytes 21626884
  171.1 3.8 copy-start.1
  171.1 3.8 copy-start.2
  269.7 126.1 %reduce-scatter.6.cloned.1.call-start = ((), (), s32[]{:S(2)}) async-start(), calls=%async_computation.6 | async-start | bytes 2703360 | tf_op jit(solution)/shard_map/reduce_scatter | solution.py:23
  403.0 162.1 %all-to-all-start = ((bf16[16,11,32,640]{3,2,1,0:T(8,128)(2,1)}), bf16[16,11,32,640]{3,2,1,0:T(8,128)(2,1)}, u32[]{:S(2)}, u32[]{:S(2)}) async-start(bf16[16,11,32,640]{3,2,1,0:T(8,128)(2,1)} %stack.2), calls=%async_computation.2 | async-start | bytes 14417920 | tf_op jit(solution)/shard_map/all_to_all | solution.py:143
  410.4 5.2 copy-start.5
  410.4 119.6 %reduce-scatter.8.cloned.1.call-start = ((), (), s32[]{:S(2)}) async-start(), calls=%async_computation.7 | async-start | bytes 2785280 | tf_op jit(solution)/shard_map/reduce_scatter | solution.py:29
Sparse Core Ops, SparseCore 0:
  9.7 149.1 all-gather.1
  269.8 92.6 reduce-scatter.3
  364.9 30.7 reduce-scatter.5
  415.7 114.1 reduce-scatter.7
